TPU v7x, 32 devices: a whole 2x2x4 slice. The times are simulated.
32 devices in a mesh: src: 4 (over z), rcv: 8 (over y, x, core).
Axes of the slice: x: 2, y: 2, z: 4, core: 2. Of those that a mesh axis runs over, the one named last changes fastest.
Arguments:
- traces: bfloat16 [512, 2048, 512], P('src', 'rcv'), may hold values from -6 to 6
- virtual_source_index: int32 [256], replicated, may hold values from 0 to 2047
Outputs:
- correlations: float32 [256, 2048, 512], P('rcv', 'src')
Inputs may be any that keep to these rules, and one draw needn't show every extreme that they name: `virtual_source_index`: receiver numbers; a receiver may be listed more than once.
All inputs are finite; a program needn't handle non-finite values.
Results may differ from a plain program's by a relative error of at most 0.0064.
Values may be sent and summed in bfloat16 or wider, within the bound.
No kernel may reach another device: no remote copies, remote signals or barrier semaphores. Data moves between devices by JAX's collectives and lax.ppermute only.
A program may use at most 192 MiB of HBM per device.

v0:
```python
import math

import jax
import jax.numpy as jnp
from jax import lax
from jax.sharding import PartitionSpec as P

NF = 128


def make_tables(times_count):
    freqs = jnp.arange(NF, dtype=jnp.int32)
    times = jnp.arange(times_count, dtype=jnp.int32)
    phase = (freqs[:, None] * times[None, :] % times_count).astype(jnp.float32) * (
        2.0 * math.pi / times_count
    )
    basis = jnp.stack([jnp.cos(phase), -jnp.sin(phase)], axis=1)
    forward = (basis / jnp.sqrt(jnp.float32(times_count))).astype(jnp.bfloat16)
    inverse = (basis / jnp.sqrt(jnp.float32(NF))).astype(jnp.bfloat16)
    return (forward, inverse)


def complex_gram(left_operand, right_operand):
    real_part = jnp.einsum(
        "ekg,ekh->egh", left_operand[:, 0], right_operand[:, 0], preferred_element_type=jnp.float32
    ) + jnp.einsum(
        "ekg,ekh->egh", left_operand[:, 1], right_operand[:, 1], preferred_element_type=jnp.float32
    )
    imaginary_part = jnp.einsum(
        "ekg,ekh->egh", left_operand[:, 0], right_operand[:, 1], preferred_element_type=jnp.float32
    ) - jnp.einsum(
        "ekg,ekh->egh", left_operand[:, 1], right_operand[:, 0], preferred_element_type=jnp.float32
    )
    return jnp.stack([real_part, imaginary_part], axis=1)


def shards(traces, virtual_source_index):
    shots_here, rcv_here, times_count = traces.shape
    forward, inverse = make_tables(times_count)
    spectra = jnp.einsum(
        "kt,srt->ksr",
        forward.reshape(2 * NF, times_count),
        traces,
        preferred_element_type=jnp.float32,
    )
    spectra = spectra.astype(jnp.bfloat16).reshape(NF, 2, shots_here, rcv_here)
    spectra = lax.all_to_all(spectra, "rcv", split_axis=0, concat_axis=3, tiled=True)
    rows = jnp.take(spectra, virtual_source_index, axis=3)
    total_shots = shots_here * lax.axis_size("src")
    columns = lax.all_to_all(spectra, "src", split_axis=3, concat_axis=2, tiled=True)
    gram = complex_gram(lax.all_gather(rows, "src", axis=2, tiled=True), columns)
    scaled = (gram * (1.0 / jnp.sqrt(jnp.float32(total_shots)))).astype(jnp.bfloat16)
    inverse_flattened = inverse.reshape(2 * NF, times_count)
    block = lax.all_to_all(scaled, "rcv", split_axis=2, concat_axis=0, tiled=True)
    folded = block.reshape(2 * NF, block.shape[2], block.shape[3])
    return jnp.einsum("kt,kvr->vrt", inverse_flattened, folded, preferred_element_type=jnp.float32)


def solution(mesh):
    placed = (P("src", "rcv", None), P())
    return jax.shard_map(
        shards, mesh=mesh, in_specs=placed, out_specs=P("rcv", "src", None), check_vma=False
    )
```

profile of v0, /device:TPU:0, one launch (start us, length us, event | category | flops | bytes accessed | tf_op | source)
XLA Modules:
  0.0 1035.7 jit_solution(696779018619299867)
XLA Ops:
  6.5 1.0 sine_negate_fusion
  7.6 0.1 multiply_convert_fusion.1
  7.7 0.3 copy.47
  7.9 0.1 reshape.106
  8.1 19.0 %convolution_convert_fusion = bf16[256,128,256]{2,0,1:T(8,128)(2,1)} fusion(bf16[256,512,1]{1,0,2:T(8,128)(2,1)S(1)} %reshape.106, bf16[128,256,512]{2,1,0:T(8,128)(2,1)} %param.2), kind=kOutput, calls=%fused_computation.3 | convolution fusion | flops 8598323200 | bytes 50593792 | tf_op jit(solution)/shard_map/kt,srt->ksr/dot_general | solution.py:40
  27.0 15.9 %copy.60 = bf16[256,128,256]{2,1,0:T(8,128)(2,1)S(1)} copy(bf16[256,128,256]{2,0,1:T(8,128)(2,1)} %convolution_convert_fusion) | data formatting | bytes 33554432 | tf_op jit(solution)/shard_map/reshape | solution.py:46
  42.9 189.0 %all_to_all.51 = bf16[128,2,128,256]{3,2,1,0:T(8,128)(2,1)} all-to-all(bf16[128,2,128,256]{3,2,1,0:T(8,128)(2,1)S(1)} %bitcast.53), channel_id=1, replica_groups=mesh['src'=4,'rcv'=8] {'rcv'}, dimensions={0} | all-to-all | bytes 33554432 | tf_op jit(solution)/shard_map/all_to_all | solution.py:47
  231.9 21.6 %copy.49 = bf16[16,2,128,8,256]{2,4,3,1,0:T(8,128)(2,1)} copy(bf16[16,2,128,8,256]{4,2,1,0,3:T(8,128)(2,1)} %bitcast.51) | data formatting | bytes 33554432 | tf_op jit(solution)/shard_map/all_to_all | solution.py:47
  253.4 31.0 %copy.52 = bf16[16,2,128,2048]{2,1,0,3:T(2,128)(2,1)} copy(bf16[16,2,128,2048]{2,3,1,0:T(8,128)(2,1)} %bitcast.55) | data formatting | bytes 33554432 | tf_op jit(solution)/shard_map/all_to_all | solution.py:47
  284.4 0.0 copy-start.1
  284.4 7.1 all-to-all-start.1
  291.5 0.2 all-gather.2.cloned.1.call-start
  291.7 0.0 copy-done.1
  291.8 23.3 %copy.61 = bf16[16,2,128,8,256]{2,0,4,3,1:T(8,128)(2,1)} copy(bf16[16,2,128,8,256]{4,2,1,0,3:T(8,128)(2,1)} %bitcast.52) | data formatting | bytes 33554432 | tf_op jit(solution)/shard_map/all_to_all | solution.py:47
  315.1 6.8 gather_fusion
  322.0 2.4 fusion.7
  324.4 0.0 all-gather.2.cloned.1.call-update
  324.4 464.7 %all-to-all-done.1 = bf16[16,2,128,2048]{2,1,0,3:T(2,128)(2,1)} async-done(((bf16[16,2,128,2048]{2,1,0,3:T(2,128)(2,1)}), bf16[16,2,128,2048]{2,1,0,3:T(2,128)(2,1)}, u32[]{:S(2)}, u32[]{:S(2)}) %all-to-all-start.1) | async-done | bytes 16777248 | tf_op jit(solution)/shard_map/all_to_all | solution.py:50
  789.1 15.2 %copy.53 = bf16[16,2,128,2048]{2,3,1,0:T(8,128)(2,1)} copy(bf16[16,2,128,2048]{2,1,0,3:T(2,128)(2,1)} %all-to-all-done.1) | data formatting | bytes 33554432 | tf_op jit(solution)/shard_map/all_to_all | solution.py:50
  804.2 22.4 %copy.54 = bf16[16,2,4,128,512]{4,3,2,0,1:T(8,128)(2,1)} copy(bf16[16,2,4,128,512]{3,4,2,1,0:T(8,128)(2,1)} %bitcast.54) | data formatting | bytes 33554432 | tf_op jit(solution)/shard_map/all_to_all | solution.py:50
  826.6 0.0 all-gather.2.cloned.1.call-done
  826.6 0.0 copy-start
  826.6 11.4 %fusion.3 = f32[16,256,512]{2,1,0:T(8,128)} fusion(bf16[16,2,512,512]{3,2,0,1:T(8,128)(2,1)} %bitcast.47, bf16[16,2,512,256]{2,3,0,1:T(8,128)(2,1)} %all-gather.2.cloned.1.call-done), kind=kOutput, calls=%fused_computation.10 | convolution fusion | flops 2147483648 | bytes 20971520 | tf_op jit(solution)/shard_map/ekg,ekh->egh/dot_general | solution.py:31
  838.0 1.0 copy-done
  839.1 6.8 fusion.4
  845.9 9.3 subtract_bitcast_fusion
  855.2 12.7 %add_bitcast_fusion = f32[16,1,256,512]{3,2,0,1:T(8,128)} fusion(f32[16,256,512]{2,1,0:T(8,128)} %fusion.4, bf16[16,2,512,512]{3,2,0,1:T(8,128)(2,1)} %bitcast.49, bf16[16,2,512,256]{2,3,0,1:T(8,128)(2,1)} %all-gather.2.cloned.1.call-done), kind=kOutput, calls=%fused_computation.9 | convolution fusion | flops 2149580800 | bytes 29360128 | tf_op jit(solution)/shard_map/ekg,ekh->egh/dot_general | solution.py:26
  867.9 8.1 fusion
  876.1 11.5 %copy.55 = bf16[16,2,256,512]{3,0,1,2:T(8,128)(2,1)} copy(bf16[16,2,256,512]{3,2,0,1:T(8,128)(2,1)} %fusion) | data formatting | bytes 16777216 | tf_op jit(solution)/shard_map/convert_element_type | solution.py:52
  887.6 4.9 all-to-all-start.2
  892.6 0.3 copy.58
  892.8 0.1 reshape.107
  892.9 93.6 %all-to-all-done.2 = bf16[16,2,256,512]{3,0,1,2:T(8,128)(2,1)} async-done(((bf16[16,2,256,512]{3,0,1,2:T(8,128)(2,1)}), bf16[16,2,256,512]{3,0,1,2:T(8,128)(2,1)}, u32[]{:S(2)}, u32[]{:S(2)}) %all-to-all-start.2) | async-done | bytes 8388640 | tf_op jit(solution)/shard_map/all_to_all | solution.py:54
  986.6 11.9 %copy.57 = bf16[8,16,2,32,512]{4,3,2,1,0:T(8,128)(2,1)} copy(bf16[8,16,2,32,512]{4,1,2,3,0:T(8,128)(2,1)} %bitcast.17) | data formatting | bytes 16777216 | tf_op jit(solution)/shard_map/all_to_all | solution.py:54
  998.5 29.9 %fusion.1 = f32[32,512,512]{2,1,0:T(8,128)} fusion(bf16[256,512,1]{1,0,2:T(8,128)(2,1)S(1)} %reshape.107, bf16[256,32,512]{2,1,0:T(8,128)(2,1)} %bitcast.56), kind=kOutput, calls=%fused_computation.6 | convolution fusion | flops 4294967296 | bytes 42205184 | tf_op jit(solution)/shard_map/kt,kvr->vrt/dot_general | solution.py:56
  (3 shorter events, 0.0 us)
Async XLA Ops:
  284.4 7.4 copy-start.1
  284.4 504.7 %all-to-all-start.1 = ((bf16[16,2,128,2048]{2,1,0,3:T(2,128)(2,1)}), bf16[16,2,128,2048]{2,1,0,3:T(2,128)(2,1)}, u32[]{:S(2)}, u32[]{:S(2)}) async-start(bf16[16,2,128,2048]{2,1,0,3:T(2,128)(2,1)} %copy.52), calls=%async_computation.1 | async-start | bytes 33554432 | tf_op jit(solution)/shard_map/all_to_all | solution.py:50
  291.5 535.1 %all-gather.2.cloned.1.call-start = ((), (), s32[]{:S(2)}) async-start(), calls=%async_computation.3 | async-start | bytes 10485760 | tf_op jit(solution)/shard_map/all_gather | solution.py:51
  826.6 12.4 %copy-start = (bf16[16,2,4,128,512]{4,3,2,0,1:T(8,128)(2,1)S(1)}, bf16[16,2,4,128,512]{4,3,2,0,1:T(8,128)(2,1)}, u32[]{:S(2)}) copy-start(bf16[16,2,4,128,512]{4,3,2,0,1:T(8,128)(2,1)} %copy.54) | copy-start | bytes 50331652
  887.6 99.0 %all-to-all-start.2 = ((bf16[16,2,256,512]{3,0,1,2:T(8,128)(2,1)}), bf16[16,2,256,512]{3,0,1,2:T(8,128)(2,1)}, u32[]{:S(2)}, u32[]{:S(2)}) async-start(bf16[16,2,256,512]{3,0,1,2:T(8,128)(2,1)} %copy.55), calls=%async_computation.2 | async-start | bytes 16777216 | tf_op jit(solution)/shard_map/all_to_all | solution.py:54
Sparse Core Ops, SparseCore 0:
  324.5 300.9 all-gather.1
where the time goes:
time: 1040 us
  waiting for transfers between devices  558 us (54%)
  blocking collectives  189 us (18%)
  local copies, waits for them, and re-layouts  161 us (15%)
  matrix products  89.1 us (9%)
  between operations  14 us (1%)
  starting transfers between devices  12.3 us (1%)
  other arithmetic  11.7 us (1%)
    all_to_all x1, waiting for transfers between devices, shards(): lax.all_to_all(spectra, 'src', split_axis=3, concat_axis=2, tiled=True)  465 us
    all_to_all x1, blocking collectives, shards(): lax.all_to_all(spectra, 'rcv', split_axis=0, concat_axis=3, tiled=True)  189 us
    all_to_all x1, waiting for transfers between devices, shards(): lax.all_to_all(scaled, 'rcv', split_axis=2, concat_axis=0, tiled=True)  93.6 us
    all_to_all x3, local copies, waits for them, and re-layouts, shards(): lax.all_to_all(spectra, 'rcv', split_axis=0, concat_axis=3, tiled=True)  75.9 us
    all_to_all x2, local copies, waits for them, and re-layouts, shards(): lax.all_to_all(spectra, 'src', split_axis=3, concat_axis=2, tiled=True)  37.6 us
    dot_general x1, matrix products, shards(): jnp.einsum('kt,kvr->vrt', inverse_flattened, folded, preferred_element_ty...  29.9 us
  transfers between devices with their start and end apart: 3, of which 2 were waited for; matrix products, arithmetic and copies ran while one was open for 7% of the time, Pallas kernels for 0%

commit v1 on v0

v1 whole, which is shorter than its diff:
```python
import functools
import math

import jax
import jax.numpy as jnp
from jax import lax
from jax.experimental import pallas as pl
from jax.experimental.pallas import tpu as pltpu
from jax.sharding import PartitionSpec as P


NF = 128


def make_tables(times_count):
    freqs = jnp.arange(NF, dtype=jnp.int32)
    times = jnp.arange(times_count, dtype=jnp.int32)
    phase = (freqs[:, None] * times[None, :] % times_count).astype(jnp.float32) * (
        2.0 * math.pi / times_count
    )
    basis = jnp.stack([jnp.cos(phase), -jnp.sin(phase)], axis=1)
    forward = (basis / jnp.sqrt(jnp.float32(times_count))).astype(jnp.bfloat16)
    inverse = (basis / jnp.sqrt(jnp.float32(NF))).astype(jnp.bfloat16)
    return (forward, inverse)


def left_operands(rows):
    return jnp.concatenate(
        [
            jnp.concatenate([rows[0], rows[1]], axis=1),
            jnp.concatenate([-rows[1], rows[0]], axis=1),
        ],
        axis=0,
    )


def gram_body(scale, sources, *refs):
    rows, cols, out = refs[:sources], refs[sources : 2 * sources], refs[-1]
    left = [left_operands(r) for r in rows]
    per, _, shots, rcv = cols[0].shape
    owners, _, _, vs, _ = out.shape
    for h in range(per):
        total = None
        for a, c in zip(left, cols):
            part = jnp.dot(a, c[h].reshape(2 * shots, rcv), preferred_element_type=jnp.float32)
            total = part if total is None else total + part
        total = (total * scale).astype(out.dtype)
        for c in range(2):
            for o in range(owners):
                at = (c * owners + o) * vs
                out[o, 0, c, :, h * rcv : (h + 1) * rcv] = total[at : at + vs]


def gram(rows, cols, owners, scale):
    k, vs, shots = rows[0].shape
    per, _, _, rcv = cols[0].shape
    flops = len(rows) * 2 * (2 * vs) * shots * per * rcv * k
    moved = len(rows) * 2 * k * shots * (vs + per * rcv) + 2 * k * vs * per * rcv
    return pl.pallas_call(
        functools.partial(gram_body, scale, len(rows)),
        grid=(k // 2,),
        in_specs=[pl.BlockSpec((2, vs, shots), lambda f: (f, 0, 0))] * len(rows)
        + [pl.BlockSpec((per, 2, shots, rcv), lambda f: (0, f, 0, 0))] * len(rows),
        out_specs=pl.BlockSpec((owners, 1, 2, vs // owners, per * rcv), lambda f: (0, f, 0, 0, 0)),
        out_shape=jax.ShapeDtypeStruct((owners, k // 2, 2, vs // owners, per * rcv), jnp.bfloat16),
        cost_estimate=pl.CostEstimate(flops=flops, bytes_accessed=moved, transcendentals=0),
        name="gram",
    )(*rows, *cols)


def lags_body(pieces, *refs):
    table, out = refs[pieces], refs[-1]
    for v in range(out.shape[0]):
        spectra = jnp.concatenate([refs[p][v] for p in range(pieces)], axis=0)
        out[v] = lax.dot_general(
            spectra, table[...], (((0,), (0,)), ((), ())), preferred_element_type=jnp.float32
        )


def lags(pieces, table):
    vs, _, rcv = pieces[0].shape
    k, times = table.shape
    step = 2
    return pl.pallas_call(
        functools.partial(lags_body, len(pieces)),
        grid=(vs // step,),
        in_specs=[pl.BlockSpec((step,) + p.shape[1:], lambda v: (v, 0, 0)) for p in pieces]
        + [pl.BlockSpec((k, times), lambda v: (0, 0))],
        out_specs=pl.BlockSpec((step, rcv, times), lambda v: (v, 0, 0)),
        out_shape=jax.ShapeDtypeStruct((vs, rcv, times), jnp.float32),
        cost_estimate=pl.CostEstimate(
            flops=2 * vs * rcv * times * k,
            bytes_accessed=2 * vs * rcv * k + 4 * vs * rcv * times,
            transcendentals=0,
        ),
        name="lags",
    )(*pieces, table)


def signed_product(left, cols, h):
    _, _, shots, rcv = cols.shape
    return jnp.dot(left, cols[h].reshape(2 * shots, rcv), preferred_element_type=jnp.float32)


def cross_body(scale, sel, own_rows, end_rows, own_cols, end_cols, out):
    rcv = own_cols.shape[3]
    own, end = left_operands(own_rows), left_operands(end_rows)
    for h in range(own_cols.shape[0]):
        total = signed_product(own, own_cols, h) + signed_product(end, end_cols, h)
        out[0, 0, :, h * rcv : (h + 1) * rcv] = (total * scale).astype(out.dtype)


def cross(sel, own_rows, end_rows, own_cols, end_cols, per, scale):
    k, vs, shots = own_rows.shape
    rcv = own_cols.shape[3]
    rows = pl.BlockSpec((2, vs, shots), lambda f, m, sel: (f, 0, 0))
    return pl.pallas_call(
        functools.partial(cross_body, scale),
        grid_spec=pltpu.PrefetchScalarGridSpec(
            num_scalar_prefetch=1,
            grid=(k // 2, 2),
            in_specs=[
                rows,
                rows,
                pl.BlockSpec((per, 2, shots, rcv), lambda f, m, sel: (2 * sel[0] + m, f, 0, 0)),
                pl.BlockSpec((per, 2, shots, rcv), lambda f, m, sel: (sel[0] + m, f, 0, 0)),
            ],
            out_specs=pl.BlockSpec((1, 1, 2 * vs, per * rcv), lambda f, m, sel: (m, f, 0, 0)),
        ),
        out_shape=jax.ShapeDtypeStruct((2, k // 2, 2 * vs, per * rcv), jnp.bfloat16),
        cost_estimate=pl.CostEstimate(
            flops=16 * k * vs * shots * per * rcv,
            bytes_accessed=4 * k * (vs * shots + 2 * shots * per * rcv + vs * per * rcv),
            transcendentals=0,
        ),
        name="cross",
    )(sel, own_rows, end_rows, own_cols, end_cols)


def onward_body(scale, sel, own_rows, own_cols, far, out):
    rcv = own_cols.shape[3]
    own = left_operands(own_rows)
    for h in range(own_cols.shape[0]):
        at = slice(h * rcv, (h + 1) * rcv)
        total = signed_product(own, own_cols, h) * scale + far[0, 0, :, at].astype(jnp.float32)
        out[0, :, at] = total.astype(out.dtype)


def onward(sel, own_rows, own_cols, crossed, per, scale):
    k, vs, shots = own_rows.shape
    rcv = own_cols.shape[3]
    return pl.pallas_call(
        functools.partial(onward_body, scale),
        grid_spec=pltpu.PrefetchScalarGridSpec(
            num_scalar_prefetch=1,
            grid=(k // 2,),
            in_specs=[
                pl.BlockSpec((2, vs, shots), lambda f, sel: (f, 0, 0)),
                pl.BlockSpec((per, 2, shots, rcv), lambda f, sel: (3 - 3 * sel[0], f, 0, 0)),
                pl.BlockSpec((1, 1, 2 * vs, per * rcv), lambda f, sel: (1 - sel[0], f, 0, 0)),
            ],
            out_specs=pl.BlockSpec((1, 2 * vs, per * rcv), lambda f, sel: (f, 0, 0)),
        ),
        out_shape=jax.ShapeDtypeStruct((k // 2, 2 * vs, per * rcv), jnp.bfloat16),
        cost_estimate=pl.CostEstimate(
            flops=4 * k * vs * shots * per * rcv,
            bytes_accessed=2 * k * (vs * shots + shots * per * rcv + 2 * vs * per * rcv),
            transcendentals=0,
        ),
        name="onward",
    )(sel, own_rows, own_cols, crossed)


def finish_body(scale, sel, own_rows, end_rows, own_cols, end_cols, near, mine, arrived, out):
    owners, _, _, vs, _ = out.shape
    rcv = own_cols.shape[3]

    def put(h, total):
        total = total.astype(out.dtype)
        for c in range(2):
            for o in range(owners):
                at = (c * owners + o) * vs
                out[o, 0, c, :, h * rcv : (h + 1) * rcv] = total[at : at + vs]

    @pl.when(sel[2] == 1)
    def _():
        own, end = left_operands(own_rows), left_operands(end_rows)
        for h in range(own_cols.shape[0]):
            total = signed_product(own, own_cols, h) + signed_product(end, end_cols, h)
            at = slice(h * rcv, (h + 1) * rcv)
            put(h, total * scale + near[0, 0, :, at].astype(jnp.float32))

    @pl.when(sel[2] == 0)
    def _():
        for h in range(own_cols.shape[0]):
            at = slice(h * rcv, (h + 1) * rcv)
            put(h, mine[0, :, at].astype(jnp.float32) + arrived[0, :, at].astype(jnp.float32))


def finish(sel, own_rows, end_rows, own_cols, end_cols, crossed, mine, arrived, per, owners, scale):
    k, vs, shots = own_rows.shape
    rcv = own_cols.shape[3]
    rows = pl.BlockSpec((2, vs, shots), lambda f, sel: (f, 0, 0))
    partial = pl.BlockSpec((1, 2 * vs, per * rcv), lambda f, sel: (f, 0, 0))
    return pl.pallas_call(
        functools.partial(finish_body, scale),
        grid_spec=pltpu.PrefetchScalarGridSpec(
            num_scalar_prefetch=1,
            grid=(k // 2,),
            in_specs=[
                rows,
                rows,
                pl.BlockSpec((per, 2, shots, rcv), lambda f, sel: (sel[1], f, 0, 0)),
                pl.BlockSpec((per, 2, shots, rcv), lambda f, sel: (2 - 2 * sel[0], f, 0, 0)),
                pl.BlockSpec((1, 1, 2 * vs, per * rcv), lambda f, sel: (sel[0], f, 0, 0)),
                partial,
                partial,
            ],
            out_specs=pl.BlockSpec(
                (owners, 1, 2, vs // owners, per * rcv), lambda f, sel: (0, f, 0, 0, 0)
            ),
        ),
        out_shape=jax.ShapeDtypeStruct((owners, k // 2, 2, vs // owners, per * rcv), jnp.bfloat16),
        cost_estimate=pl.CostEstimate(
            flops=8 * k * vs * shots * per * rcv,
            bytes_accessed=2 * k * (2 * vs * shots + 2 * shots * per * rcv + 4 * vs * per * rcv),
            transcendentals=0,
        ),
        name="finish",
    )(sel, own_rows, end_rows, own_cols, end_cols, crossed, mine, arrived)


def gram_by_cycle(rows, sp, per, n_src, n_rcv, scale):
    at = lax.axis_index("src")
    spread = lax.all_gather(rows, "src", axis=0, tiled=False)
    here = [rows]
    cols = [lax.dynamic_slice_in_dim(sp, at * per, per, 0)]
    for d in range(1, n_src):
        here.append(lax.dynamic_index_in_dim(spread, lax.rem(at + n_src - d, n_src), 0, False))
        block = lax.dynamic_slice_in_dim(sp, lax.rem(at + d, n_src) * per, per, 0)
        cols.append(lax.ppermute(block, "src", [(s, (s + d) % n_src) for s in range(n_src)]))
    return gram(here, cols, n_rcv, scale)


def gram_by_halves(rows, sp, per, n_rcv, scale):
    at = lax.axis_index("src")
    low = (at < 2).astype(jnp.int32)
    inner = ((at == 1) | (at == 2)).astype(jnp.int32)
    sel = jnp.stack([low, at.astype(jnp.int32), inner])
    inward = [(0, 1), (3, 2)]
    block = lax.dynamic_slice_in_dim(sp, low * per, 3 * per, 0)
    end_rows = lax.ppermute(rows, "src", inward)
    end_cols = lax.ppermute(block, "src", inward)
    crossed = cross(sel, rows, end_rows, sp, end_cols, per, scale)
    crossed = lax.ppermute(crossed, "src", [(1, 2), (2, 1)])
    mine = onward(sel, rows, sp, crossed, per, scale)
    arrived = lax.ppermute(mine, "src", [(1, 0), (2, 3)])
    return finish(
        sel, rows, end_rows, sp, end_cols, crossed, mine, arrived, per, n_rcv, scale
    )


def chunk_sizes(count):
    return [1] * (count % 2) + ([2] * (count // 2) if count < 8 else [1, 1] + [2] * (count // 2 - 2) + [1, 1])


def shards(traces, index):
    shots, rcv, times = traces.shape
    n_rcv = lax.axis_size("rcv")
    n_src = lax.axis_size("src")
    per = n_rcv // n_src
    vs = index.shape[0]
    scale = 1.0 / math.sqrt(shots * n_src)
    forward, inverse = make_tables(times)
    places = jnp.arange(n_rcv * rcv, dtype=jnp.int32).reshape(n_rcv, 1, rcv)
    hot = (index[None, :, None] == places).astype(jnp.bfloat16)
    spectra = jnp.einsum(
        "kt,srt->ksr", forward.reshape(2 * NF, times), traces, preferred_element_type=jnp.float32
    ).astype(jnp.bfloat16)
    pieces = []
    start = 0
    for fc in chunk_sizes(NF // n_rcv):
        count = n_rcv * 2 * fc
        sp = spectra[start : start + count].reshape(n_rcv, 2 * fc, shots, rcv)
        start += count
        sp = lax.all_to_all(sp, "rcv", split_axis=0, concat_axis=0, tiled=True)
        rows = jnp.einsum("jvr,jksr->kvs", hot, sp, preferred_element_type=jnp.float32)
        rows = rows.astype(jnp.bfloat16)
        if n_src == 4:
            g = gram_by_halves(rows, sp, per, n_rcv, scale)
        else:
            g = gram_by_cycle(rows, sp, per, n_src, n_rcv, scale)
        g = lax.all_to_all(g, "rcv", split_axis=0, concat_axis=0, tiled=True)
        pieces.append(g.reshape(count, vs // n_rcv, per * rcv).transpose(1, 0, 2))
    return lags(pieces, inverse.reshape(2 * NF, times))


def solution(mesh):
    placed = (P("src", "rcv", None), P())

    return jax.shard_map(
        shards, mesh=mesh, in_specs=placed, out_specs=P("rcv", "src", None), check_vma=False
    )
```

time: 1040 us -> 804 us (0.77)
  waiting for transfers between devices: 558 us -> 284 us
  starting transfers between devices: 12.3 us -> 246 us
  blocking collectives: 189 us -> 0 us
  Pallas kernels: 0 us -> 134 us
  local copies, waits for them, and re-layouts: 161 us -> 90.7 us
  matrix products: 89.1 us -> 32.4 us
  between operations: 14 us -> 0.96 us
    all_to_all x2 -> x20, waiting for transfers between devices: 558 us -> 116 us  [the longest x10 114 us: shards(): sp = lax.all_to_all(sp, 'rcv', split_axis=0, concat_axis=0, tiled=True)]
    all_to_all x1 -> x0, blocking collectives: 189 us -> none  [shards(): lax.all_to_all(spectra, 'rcv', split_axis=0, concat_axis=3, tiled=True)]
    ppermute x0 -> x40, waiting for transfers between devices: none -> 168 us  [the longest x10 108 us: gram_by_halves(): end_rows = lax.ppermute(rows, 'src', inward)]
    ppermute x0 -> x40, starting transfers between devices: none -> 168 us  [the longest x10 101 us: gram_by_halves(): end_cols = lax.ppermute(block, 'src', inward)]
    pallas_call x0 -> x31, Pallas kernels: none -> 134 us  [the longest x10 46.8 us: cross(): pl.pallas_call(functools.partial(cross_body, scale), grid_spec=pltpu.Pref...]
    all_to_all x6 -> x0, local copies, waits for them, and re-layouts: 125 us -> none  [the longest x3 75.9 us: shards(): lax.all_to_all(spectra, 'rcv', split_axis=0, concat_axis=3, tiled=True)]
    all_to_all x2 -> x20, starting transfers between devices: 12.1 us -> 78.6 us  [the longest x10 39.5 us: shards(): sp = lax.all_to_all(sp, 'rcv', split_axis=0, concat_axis=0, tiled=True)]
    dot_general x6 -> x11, matrix products: 89.1 us -> 32.4 us  [the longest x1 19 us: shards(): jnp.einsum('kt,srt->ksr', forward.reshape(2 * NF, times), traces, preferr...]
  transfers between devices with their start and end apart: 3 -> 60, of which waited for: 2 -> 21; matrix products, arithmetic and copies ran while one was open for 7% -> 11% of each run, Pallas kernels for 0% -> 15%
where the time goes in v1:
time: 804 us; the launch traced here: 791 us
  waiting for transfers between devices  284 us (35%)
  starting transfers between devices  246 us (31%)
  Pallas kernels  134 us (17%)
  local copies, waits for them, and re-layouts  90.7 us (11%)
  matrix products  32.4 us (4%)
    all_to_all x10, waiting for transfers between devices, shards(): sp = lax.all_to_all(sp, 'rcv', split_axis=0, concat_axis=0, tiled=True)  114 us
    ppermute x10, waiting for transfers between devices, gram_by_halves(): end_rows = lax.ppermute(rows, 'src', inward)  108 us
    ppermute x10, starting transfers between devices, gram_by_halves(): end_cols = lax.ppermute(block, 'src', inward)  101 us
    ppermute x10, waiting for transfers between devices, gram_by_halves(): arrived = lax.ppermute(mine, 'src', [(1, 0), (2, 3)])  60.3 us
    pallas_call x10, Pallas kernels, cross(): pl.pallas_call(functools.partial(cross_body, scale), grid_spec=pltpu.Pref...  46.8 us
    slice x12, local copies, waits for them, and re-layouts, shards(): sp = spectra[start:start + count].reshape(n_rcv, 2 * fc, shots, rcv)  40.7 us
    all_to_all x10, starting transfers between devices, shards(): sp = lax.all_to_all(sp, 'rcv', split_axis=0, concat_axis=0, tiled=True)  39.5 us
    all_to_all x10, starting transfers between devices, shards(): g = lax.all_to_all(g, 'rcv', split_axis=0, concat_axis=0, tiled=True)  39.2 us
  transfers between devices with their start and end apart: 60, of which 21 were waited for; matrix products, arithmetic and copies ran while one was open for 11% of the time, Pallas kernels for 15%

profile of v1, /device:TPU:0, one launch (start us, length us, event | category | flops | bytes accessed | tf_op | source)
XLA Modules:
  0.0 791.5 jit_solution(13964005557454703877)
XLA Ops:
  2.2 19.0 %convolution_convert_fusion = bf16[256,128,256]{2,0,1:T(8,128)(2,1)} fusion(bf16[256,512,1]{1,0,2:T(8,128)(2,1)S(1)} %reshape.185, bf16[128,256,512]{2,1,0:T(8,128)(2,1)} %param.2), kind=kOutput, calls=%fused_computation | convolution fusion | flops 8598323200 | bytes 50593792 | tf_op jit(solution)/shard_map/kt,srt->ksr/dot_general | solution.py:277
  21.2 3.6 fusion.147
  26.1 5.2 all-to-all-start.18
  33.9 12.8 %all-to-all-done.18.own_cols = bf16[8,2,128,256]{3,2,1,0:T(8,128)(2,1)S(1)} async-done(((bf16[8,2,128,256]{3,2,1,0:T(8,128)(2,1)}), bf16[8,2,128,256]{3,2,1,0:T(8,128)(2,1)S(1)}, u32[]{:S(2)}, u32[]{:S(2)}) %all-to-all-start.18) | async-done | bytes 1048608 | tf_op jit(solution)/shard_map/all_to_all | solution.py:286
  52.6 14.0 %all-to-all-done.16.own_cols = bf16[8,2,128,256]{3,2,1,0:T(8,128)(2,1)S(1)} async-done(((bf16[8,2,128,256]{3,2,1,0:T(8,128)(2,1)}), bf16[8,2,128,256]{3,2,1,0:T(8,128)(2,1)S(1)}, u32[]{:S(2)}, u32[]{:S(2)}) %all-to-all-start.16) | async-done | bytes 1048608 | tf_op jit(solution)/shard_map/all_to_all | solution.py:286
  72.6 14.0 %all-to-all-done.2.own_cols = bf16[8,2,128,256]{3,2,1,0:T(8,128)(2,1)S(1)} async-done(((bf16[8,2,128,256]{3,2,1,0:T(8,128)(2,1)}), bf16[8,2,128,256]{3,2,1,0:T(8,128)(2,1)S(1)}, u32[]{:S(2)}, u32[]{:S(2)}) %all-to-all-start.2) | async-done | bytes 1048608 | tf_op jit(solution)/shard_map/all_to_all | solution.py:286
  86.5 3.6 all-to-all-start
  90.1 9.0 %fusion.148 = (bf16[32,128,256]{2,0,1:T(8,128)(2,1)S(1)}, bf16[32,128,256]{2,0,1:T(8,128)(2,1)}, bf16[32,128,256]{2,0,1:T(8,128)(2,1)}, bf16[32,128,256]{2,0,1:T...) fusion(bf16[256,128,256]{2,0,1:T(8,128)(2,1)} %convolution_convert_fusion), kind=kLoop, calls=%fused_computation.118 | loop fusion | bytes 25165824 | tf_op jit(solution)/shard_map/slice | solution.py:284
  101.6 3.8 all-to-all-done.own_cols
  105.4 3.6 all-to-all-start.14
  109.0 4.1 copy.103
  113.2 22.4 %all-to-all-done.14.own_cols = bf16[8,4,128,256]{3,2,1,0:T(8,128)(2,1)S(1)} async-done(((bf16[8,4,128,256]{3,2,1,0:T(8,128)(2,1)}), bf16[8,4,128,256]{3,2,1,0:T(8,128)(2,1)S(1)}, u32[]{:S(2)}, u32[]{:S(2)}) %all-to-all-start.14) | async-done | bytes 2097184 | tf_op jit(solution)/shard_map/all_to_all | solution.py:286
  136.9 3.6 all-to-all-start.12
  140.5 4.1 copy.100
  144.6 22.5 %all-to-all-done.12.own_cols = bf16[8,4,128,256]{3,2,1,0:T(8,128)(2,1)S(1)} async-done(((bf16[8,4,128,256]{3,2,1,0:T(8,128)(2,1)}), bf16[8,4,128,256]{3,2,1,0:T(8,128)(2,1)S(1)}, u32[]{:S(2)}, u32[]{:S(2)}) %all-to-all-start.12) | async-done | bytes 2097184 | tf_op jit(solution)/shard_map/all_to_all | solution.py:286
  168.4 4.1 all-to-all-start.10
  172.5 4.1 copy.97
  176.6 22.5 %all-to-all-done.10.own_cols = bf16[8,4,128,256]{3,2,1,0:T(8,128)(2,1)S(1)} async-done(((bf16[8,4,128,256]{3,2,1,0:T(8,128)(2,1)}), bf16[8,4,128,256]{3,2,1,0:T(8,128)(2,1)S(1)}, u32[]{:S(2)}, u32[]{:S(2)}) %all-to-all-start.10) | async-done | bytes 2097184 | tf_op jit(solution)/shard_map/all_to_all | solution.py:286
  200.4 3.6 all-to-all-start.8
  204.0 4.3 copy.94
  212.3 4.4 collective-permute-start.37
  230.5 4.3 all-to-all-start.6
  238.6 4.6 collective-permute-start.29
  249.0 7.3 collective-permute-done.32.end_rows
  256.4 5.1 collective-permute-start.4
  270.2 56.4 %collective-permute-done.4.end_rows = bf16[2,256,128]{2,1,0:T(8,128)(2,1)} collective-permute-done((bf16[2,256,128]{2,1,0:T(8,128)(2,1)S(1)}, bf16[2,256,128]{2,1,0:T(8,128)(2,1)}, u32[]{:S(2)}, u32[]{:S(2)}) %collective-permute-start.4) | collective-permute-done | bytes 131104 | tf_op jit(solution)/shard_map/ppermute | solution.py:252
  328.8 5.8 collective-permute-start.28
  342.0 5.1 collective-permute-start.24
  347.9 4.4 all-to-all-start.4
  352.3 26.0 %collective-permute-done.24.end_rows = bf16[4,256,128]{2,1,0:T(8,128)(2,1)} collective-permute-done((bf16[4,256,128]{2,1,0:T(8,128)(2,1)S(1)}, bf16[4,256,128]{2,1,0:T(8,128)(2,1)}, u32[]{:S(2)}, u32[]{:S(2)}) %collective-permute-start.24) | collective-permute-done | bytes 262176 | tf_op jit(solution)/shard_map/ppermute | solution.py:252
  378.3 5.2 collective-permute-start.20
  386.7 4.5 collective-permute-start.16
  396.3 5.5 cross.17
  411.0 7.2 collective-permute-start.21
  422.4 5.5 cross.16
  435.4 60.6 %collective-permute-start.17 = (bf16[6,4,128,256]{3,2,1,0:T(8,128)(2,1)}, bf16[6,4,128,256]{3,2,1,0:T(8,128)(2,1)}, u32[]{:S(2)}, u32[]{:S(2)}) collective-permute-start(bf16[6,4,128,256]{3,2,1,0:T(8,128)(2,1)} %constant_dynamic-slice_fusion.5), channel_id=1, source_target_pairs={{0,8},{24,16},{1,9},{25,17},{2,10},{26,18},{3,11},{27,19},{4,12},{... | collective-permute-start | bytes 4718600 | tf_op jit(solution)/shard_map/ppermute | solution.py:253
  499.2 3.6 all-to-all-start.19
  514.6 4.2 all-to-all-start.17
  518.8 5.4 cross.15
  533.5 9.0 %collective-permute-start.13 = (bf16[6,4,128,256]{3,2,1,0:T(8,128)(2,1)}, bf16[6,4,128,256]{3,2,1,0:T(8,128)(2,1)}, u32[]{:S(2)}, u32[]{:S(2)}) collective-permute-start(bf16[6,4,128,256]{3,2,1,0:T(8,128)(2,1)} %constant_dynamic-slice_fusion.6), channel_id=1, source_target_pairs={{0,8},{24,16},{1,9},{25,17},{2,10},{26,18},{3,11},{27,19},{4,12},{... | collective-permute-start | bytes 4718600 | tf_op jit(solution)/shard_map/ppermute | solution.py:253
  545.7 4.2 all-to-all-start.3
  563.1 5.5 cross.14
  573.9 7.2 collective-permute-done.12.end_rows
  585.1 6.6 collective-permute-start.9
  591.8 4.0 finish.17
  596.6 3.8 all-to-all-start.15
  600.4 5.4 cross.13
  613.8 4.0 finish.16
  617.8 4.2 all-to-all-start.13
  624.4 5.9 collective-permute-start.8
  630.3 6.2 collective-permute-done.8.end_rows
  637.2 5.4 cross.12
  648.2 4.0 finish.15
  652.2 4.2 all-to-all-start.11
  661.1 15.9 %collective-permute-done.19.arrived = bf16[2,512,512]{2,1,0:T(8,128)(2,1)} collective-permute-done((bf16[2,512,512]{2,1,0:T(8,128)(2,1)}, bf16[2,512,512]{2,1,0:T(8,128)(2,1)}, u32[]{:S(2)}, u32[]{:S(2)}) %collective-permute-start.19) | collective-permute-done | bytes 1048608 | tf_op jit(solution)/shard_map/ppermute | solution.py:257
  677.0 4.0 finish.14
  681.0 4.2 all-to-all-start.9
  691.2 7.0 collective-permute-done.15.arrived
  698.2 4.0 finish.13
  702.2 3.6 all-to-all-start.7
  705.8 36.3 %collective-permute-done.11.arrived = bf16[2,512,512]{2,1,0:T(8,128)(2,1)S(1)} collective-permute-done((bf16[2,512,512]{2,1,0:T(8,128)(2,1)}, bf16[2,512,512]{2,1,0:T(8,128)(2,1)S(1)}, u32[]{:S(2)}, u32[]{:S(2)}) %collective-permute-start.11) | collective-permute-done | bytes 1048608 | tf_op jit(solution)/shard_map/ppermute | solution.py:257
  743.0 4.0 finish.12
  747.0 3.6 all-to-all-start.5
  772.3 18.9 %lags.1 = f32[32,512,512]{2,1,0:T(8,128)} custom-call(bf16[32,16,512]{2,1,0:T(8,128)(2,1)} %bitcast.246, bf16[32,16,512]{2,1,0:T(8,128)(2,1)} %bitcast.245, bf16[32,32,512]{2,1,0:T(8,128)(2,1)} %bitcast.239, bf16[32,32,512]{2,1,0:T(8,128)(2,1)} %bitcast.238, bf16[32,32,512]{2,1,0:T(8,128)(2,1)} %bitcast.237, bf16[32,32,512]{2,1,0:T(8,128)(2,1)} %bitcast.236, ...), custom_call_target="tpu_custom_call" | custom-call | flops 4294967296 | bytes 41943040 | tf_op jit(solution)/shard_map/lags/pallas_call | solution.py:84
  (220 shorter events, 200.4 us)
Async XLA Ops:
  26.1 20.6 %all-to-all-start.18 = ((bf16[8,2,128,256]{3,2,1,0:T(8,128)(2,1)}), bf16[8,2,128,256]{3,2,1,0:T(8,128)(2,1)S(1)}, u32[]{:S(2)}, u32[]{:S(2)}) async-start(bf16[8,2,128,256]{3,2,1,0:T(8,128)(2,1)} %bitcast.51), calls=%async_computation.18 | async-start | bytes 2097152 | tf_op jit(solution)/shard_map/all_to_all | solution.py:286
  47.7 18.9 %all-to-all-start.16 = ((bf16[8,2,128,256]{3,2,1,0:T(8,128)(2,1)}), bf16[8,2,128,256]{3,2,1,0:T(8,128)(2,1)S(1)}, u32[]{:S(2)}, u32[]{:S(2)}) async-start(bf16[8,2,128,256]{3,2,1,0:T(8,128)(2,1)} %bitcast.46), calls=%async_computation.16 | async-start | bytes 2097152 | tf_op jit(solution)/shard_map/all_to_all | solution.py:286
  67.7 18.9 %all-to-all-start.2 = ((bf16[8,2,128,256]{3,2,1,0:T(8,128)(2,1)}), bf16[8,2,128,256]{3,2,1,0:T(8,128)(2,1)S(1)}, u32[]{:S(2)}, u32[]{:S(2)}) async-start(bf16[8,2,128,256]{3,2,1,0:T(8,128)(2,1)} %bitcast.10), calls=%async_computation.2 | async-start | bytes 2097152 | tf_op jit(solution)/shard_map/all_to_all | solution.py:286
  86.5 18.9 %all-to-all-start = ((bf16[8,2,128,256]{3,2,1,0:T(8,128)(2,1)}), bf16[8,2,128,256]{3,2,1,0:T(8,128)(2,1)S(1)}, u32[]{:S(2)}, u32[]{:S(2)}) async-start(bf16[8,2,128,256]{3,2,1,0:T(8,128)(2,1)} %bitcast.3), calls=%async_computation | async-start | bytes 2097152 | tf_op jit(solution)/shard_map/all_to_all | solution.py:286
  105.4 137.8 %copy-start.7 = (bf16[8,2,128,256]{3,2,1,0:T(8,128)(2,1)}, bf16[8,2,128,256]{3,2,1,0:T(8,128)(2,1)S(1)}, u32[]{:S(2)}) copy-start(bf16[8,2,128,256]{3,2,1,0:T(8,128)(2,1)S(1)} %all-to-all-done.own_cols) | copy-start | bytes 3145732
  105.4 30.2 %all-to-all-start.14 = ((bf16[8,4,128,256]{3,2,1,0:T(8,128)(2,1)}), bf16[8,4,128,256]{3,2,1,0:T(8,128)(2,1)S(1)}, u32[]{:S(2)}, u32[]{:S(2)}) async-start(bf16[8,4,128,256]{3,2,1,0:T(8,128)(2,1)} %bitcast.231), calls=%async_computation.14 | async-start | bytes 4194304 | tf_op jit(solution)/shard_map/all_to_all | solution.py:286
  136.9 30.2 %all-to-all-start.12 = ((bf16[8,4,128,256]{3,2,1,0:T(8,128)(2,1)}), bf16[8,4,128,256]{3,2,1,0:T(8,128)(2,1)S(1)}, u32[]{:S(2)}, u32[]{:S(2)}) async-start(bf16[8,4,128,256]{3,2,1,0:T(8,128)(2,1)} %bitcast.232), calls=%async_computation.12 | async-start | bytes 4194304 | tf_op jit(solution)/shard_map/all_to_all | solution.py:286
  168.4 30.6 %all-to-all-start.10 = ((bf16[8,4,128,256]{3,2,1,0:T(8,128)(2,1)}), bf16[8,4,128,256]{3,2,1,0:T(8,128)(2,1)S(1)}, u32[]{:S(2)}, u32[]{:S(2)}) async-start(bf16[8,4,128,256]{3,2,1,0:T(8,128)(2,1)} %bitcast.233), calls=%async_computation.10 | async-start | bytes 4194304 | tf_op jit(solution)/shard_map/all_to_all | solution.py:286
  200.4 30.2 %all-to-all-start.8 = ((bf16[8,4,128,256]{3,2,1,0:T(8,128)(2,1)}), bf16[8,4,128,256]{3,2,1,0:T(8,128)(2,1)S(1)}, u32[]{:S(2)}, u32[]{:S(2)}) async-start(bf16[8,4,128,256]{3,2,1,0:T(8,128)(2,1)} %bitcast.230), calls=%async_computation.8 | async-start | bytes 4194304 | tf_op jit(solution)/shard_map/all_to_all | solution.py:286
  212.3 31.9 %collective-permute-start.37 = (bf16[6,2,128,256]{3,2,1,0:T(8,128)(2,1)}, bf16[6,2,128,256]{3,2,1,0:T(8,128)(2,1)}, u32[]{:S(2)}, u32[]{:S(2)}) collective-permute-start(bf16[6,2,128,256]{3,2,1,0:T(8,128)(2,1)} %constant_dynamic-slice_fusion), channel_id=1, source_target_pairs={{0,8},{24,16},{1,9},{25,17},{2,10},{26,18},{3,11},{27,19},{4,12},{... | collective-permute-start | bytes 2359304 | tf_op jit(solution)/shard_map/ppermute | solution.py:253
  217.8 20.8 %collective-permute-start.36 = (bf16[2,256,128]{2,1,0:T(8,128)(2,1)}, bf16[2,256,128]{2,1,0:T(8,128)(2,1)}, u32[]{:S(2)}, u32[]{:S(2)}) collective-permute-start(bf16[2,256,128]{2,1,0:T(8,128)(2,1)} %fusion.117.own_rows), channel_id=1, source_target_pairs={{0,8},{24,16},{1,9},{25,17},{2,10},{26,18},{3,11},{27,19},{4,12},{... | collective-permute-start | bytes 393224 | tf_op jit(solution)/shard_map/ppermute | solution.py:252
  220.9 40.7 %collective-permute-start.33 = (bf16[6,2,128,256]{3,2,1,0:T(8,128)(2,1)}, bf16[6,2,128,256]{3,2,1,0:T(8,128)(2,1)}, u32[]{:S(2)}, u32[]{:S(2)}) collective-permute-start(bf16[6,2,128,256]{3,2,1,0:T(8,128)(2,1)} %constant_dynamic-slice_fusion.1), channel_id=1, source_target_pairs={{0,8},{24,16},{1,9},{25,17},{2,10},{26,18},{3,11},{27,19},{4,12},{... | collective-permute-start | bytes 2359304 | tf_op jit(solution)/shard_map/ppermute | solution.py:253
  223.5 32.9 %collective-permute-start.32 = (bf16[2,256,128]{2,1,0:T(8,128)(2,1)S(1)}, bf16[2,256,128]{2,1,0:T(8,128)(2,1)}, u32[]{:S(2)}, u32[]{:S(2)}) collective-permute-start(bf16[2,256,128]{2,1,0:T(8,128)(2,1)S(1)} %fusion.114.own_rows), channel_id=1, source_target_pairs={{0,8},{24,16},{1,9},{25,17},{2,10},{26,18},{3,11},{27,19},{4,12},{... | collective-permute-start | bytes 393224 | tf_op jit(solution)/shard_map/ppermute | solution.py:252
  226.4 108.2 %collective-permute-start.5 = (bf16[6,2,128,256]{3,2,1,0:T(8,128)(2,1)}, bf16[6,2,128,256]{3,2,1,0:T(8,128)(2,1)}, u32[]{:S(2)}, u32[]{:S(2)}) collective-permute-start(bf16[6,2,128,256]{3,2,1,0:T(8,128)(2,1)} %constant_dynamic-slice_fusion.8), channel_id=1, source_target_pairs={{0,8},{24,16},{1,9},{25,17},{2,10},{26,18},{3,11},{27,19},{4,12},{... | collective-permute-start | bytes 2359304 | tf_op jit(solution)/shard_map/ppermute | solution.py:253
  230.5 203.6 %copy-start = (bf16[8,4,128,256]{3,2,1,0:T(8,128)(2,1)}, bf16[8,4,128,256]{3,2,1,0:T(8,128)(2,1)S(1)}, u32[]{:S(2)}) copy-start(bf16[8,4,128,256]{3,2,1,0:T(8,128)(2,1)S(1)} %all-to-all-done.8.own_cols) | copy-start | bytes 6291460
  230.5 117.3 %all-to-all-start.6 = ((bf16[8,4,128,256]{3,2,1,0:T(8,128)(2,1)}), bf16[8,4,128,256]{3,2,1,0:T(8,128)(2,1)}, u32[]{:S(2)}, u32[]{:S(2)}) async-start(bf16[8,4,128,256]{3,2,1,0:T(8,128)(2,1)} %bitcast.229), calls=%async_computation.6 | async-start | bytes 4194304 | tf_op jit(solution)/shard_map/all_to_all | solution.py:286
  238.6 156.1 %collective-permute-start.29 = (bf16[6,4,128,256]{3,2,1,0:T(8,128)(2,1)}, bf16[6,4,128,256]{3,2,1,0:T(8,128)(2,1)}, u32[]{:S(2)}, u32[]{:S(2)}) collective-permute-start(bf16[6,4,128,256]{3,2,1,0:T(8,128)(2,1)} %constant_dynamic-slice_fusion.2), channel_id=1, source_target_pairs={{0,8},{24,16},{1,9},{25,17},{2,10},{26,18},{3,11},{27,19},{4,12},{... | collective-permute-start | bytes 4718600 | tf_op jit(solution)/shard_map/ppermute | solution.py:253
  244.2 93.7 %collective-permute-start.1 = (bf16[6,2,128,256]{3,2,1,0:T(8,128)(2,1)}, bf16[6,2,128,256]{3,2,1,0:T(8,128)(2,1)S(1)}, u32[]{:S(2)}, u32[]{:S(2)}) collective-permute-start(bf16[6,2,128,256]{3,2,1,0:T(8,128)(2,1)} %constant_dynamic-slice_fusion.9), channel_id=1, source_target_pairs={{0,8},{24,16},{1,9},{25,17},{2,10},{26,18},{3,11},{27,19},{4,12},{... | collective-permute-start | bytes 2359304 | tf_op jit(solution)/shard_map/ppermute | solution.py:253
  256.4 70.2 %collective-permute-start.4 = (bf16[2,256,128]{2,1,0:T(8,128)(2,1)S(1)}, bf16[2,256,128]{2,1,0:T(8,128)(2,1)}, u32[]{:S(2)}, u32[]{:S(2)}) collective-permute-start(bf16[2,256,128]{2,1,0:T(8,128)(2,1)S(1)} %fusion.111.own_rows), channel_id=1, source_target_pairs={{0,8},{24,16},{1,9},{25,17},{2,10},{26,18},{3,11},{27,19},{4,12},{... | collective-permute-start | bytes 393224 | tf_op jit(solution)/shard_map/ppermute | solution.py:252
  261.5 67.3 %collective-permute-start = (bf16[2,256,128]{2,1,0:T(8,128)(2,1)S(1)}, bf16[2,256,128]{2,1,0:T(8,128)(2,1)S(1)}, u32[]{:S(2)}, u32[]{:S(2)}) collective-permute-start(bf16[2,256,128]{2,1,0:T(8,128)(2,1)S(1)} %fusion.108.own_rows), channel_id=1, source_target_pairs={{0,8},{24,16},{1,9},{25,17},{2,10},{26,18},{3,11},{27,19},{4,12},{... | collective-permute-start | bytes 393224 | tf_op jit(solution)/shard_map/ppermute | solution.py:252
  268.9 69.0 %copy-start.22 = (bf16[4,256,128]{2,1,0:T(8,128)(2,1)}, bf16[4,256,128]{2,1,0:T(8,128)(2,1)S(1)}, u32[]{:S(2)}) copy-start(bf16[4,256,128]{2,1,0:T(8,128)(2,1)S(1)} %fusion.81.own_rows) | copy-start | bytes 786436
  270.2 76.9 %copy-start.2 = (bf16[8,4,128,256]{3,2,1,0:T(8,128)(2,1)S(1)}, bf16[8,4,128,256]{3,2,1,0:T(8,128)(2,1)}, u32[]{:S(2)}) copy-start(bf16[8,4,128,256]{3,2,1,0:T(8,128)(2,1)} %copy-done.1) | copy-start | bytes 6291460
  326.6 80.9 %collective-permute-start.38 = (bf16[2,1,512,512]{3,2,1,0:T(8,128)(2,1)}, bf16[2,1,512,512]{3,2,1,0:T(8,128)(2,1)}, u32[]{:S(2)}, u32[]{:S(2)}) collective-permute-start(bf16[2,1,512,512]{3,2,1,0:T(8,128)(2,1)} %cross.19), channel_id=1, source_target_pairs={{8,16},{16,8},{9,17},{17,9},{10,18},{18,10},{11,19},{19,11},{12,20... | collective-permute-start | bytes 3145736 | tf_op jit(solution)/shard_map/ppermute | solution.py:255
  328.8 12.5 %collective-permute-start.28 = (bf16[4,256,128]{2,1,0:T(8,128)(2,1)S(1)}, bf16[4,256,128]{2,1,0:T(8,128)(2,1)S(1)}, u32[]{:S(2)}, u32[]{:S(2)}) collective-permute-start(bf16[4,256,128]{2,1,0:T(8,128)(2,1)S(1)} %fusion.81.own_rows), channel_id=1, source_target_pairs={{0,8},{24,16},{1,9},{25,17},{2,10},{26,18},{3,11},{27,19},{4,12},{... | collective-permute-start | bytes 786440 | tf_op jit(solution)/shard_map/ppermute | solution.py:252
  334.6 86.5 %collective-permute-start.25 = (bf16[6,4,128,256]{3,2,1,0:T(8,128)(2,1)}, bf16[6,4,128,256]{3,2,1,0:T(8,128)(2,1)}, u32[]{:S(2)}, u32[]{:S(2)}) collective-permute-start(bf16[6,4,128,256]{3,2,1,0:T(8,128)(2,1)} %constant_dynamic-slice_fusion.3), channel_id=1, source_target_pairs={{0,8},{24,16},{1,9},{25,17},{2,10},{26,18},{3,11},{27,19},{4,12},{... | collective-permute-start | bytes 4718600 | tf_op jit(solution)/shard_map/ppermute | solution.py:253
  337.9 73.1 %collective-permute-start.34 = (bf16[2,1,512,512]{3,2,1,0:T(8,128)(2,1)}, bf16[2,1,512,512]{3,2,1,0:T(8,128)(2,1)}, u32[]{:S(2)}, u32[]{:S(2)}) collective-permute-start(bf16[2,1,512,512]{3,2,1,0:T(8,128)(2,1)} %cross.18), channel_id=1, source_target_pairs={{8,16},{16,8},{9,17},{17,9},{10,18},{18,10},{11,19},{19,11},{12,20... | collective-permute-start | bytes 3145736 | tf_op jit(solution)/shard_map/ppermute | solution.py:255
  342.0 36.3 %collective-permute-start.24 = (bf16[4,256,128]{2,1,0:T(8,128)(2,1)S(1)}, bf16[4,256,128]{2,1,0:T(8,128)(2,1)}, u32[]{:S(2)}, u32[]{:S(2)}) collective-permute-start(bf16[4,256,128]{2,1,0:T(8,128)(2,1)S(1)} %fusion.78.own_rows), channel_id=1, source_target_pairs={{0,8},{24,16},{1,9},{25,17},{2,10},{26,18},{3,11},{27,19},{4,12},{... | collective-permute-start | bytes 786440 | tf_op jit(solution)/shard_map/ppermute | solution.py:252
  347.9 151.4 %all-to-all-start.4 = ((bf16[8,4,128,256]{3,2,1,0:T(8,128)(2,1)}), bf16[8,4,128,256]{3,2,1,0:T(8,128)(2,1)}, u32[]{:S(2)}, u32[]{:S(2)}) async-start(bf16[8,4,128,256]{3,2,1,0:T(8,128)(2,1)} %bitcast.228), calls=%async_computation.4 | async-start | bytes 4194304 | tf_op jit(solution)/shard_map/all_to_all | solution.py:286
  378.3 8.4 %collective-permute-start.20 = (bf16[4,256,128]{2,1,0:T(8,128)(2,1)S(1)}, bf16[4,256,128]{2,1,0:T(8,128)(2,1)}, u32[]{:S(2)}, u32[]{:S(2)}) collective-permute-start(bf16[4,256,128]{2,1,0:T(8,128)(2,1)S(1)} %fusion.75.own_rows), channel_id=1, source_target_pairs={{0,8},{24,16},{1,9},{25,17},{2,10},{26,18},{3,11},{27,19},{4,12},{... | collective-permute-start | bytes 786440 | tf_op jit(solution)/shard_map/ppermute | solution.py:252
  386.7 15.1 %collective-permute-start.16 = (bf16[4,256,128]{2,1,0:T(8,128)(2,1)S(1)}, bf16[4,256,128]{2,1,0:T(8,128)(2,1)S(1)}, u32[]{:S(2)}, u32[]{:S(2)}) collective-permute-start(bf16[4,256,128]{2,1,0:T(8,128)(2,1)S(1)} %fusion.72.own_rows), channel_id=1, source_target_pairs={{0,8},{24,16},{1,9},{25,17},{2,10},{26,18},{3,11},{27,19},{4,12},{... | collective-permute-start | bytes 786440 | tf_op jit(solution)/shard_map/ppermute | solution.py:252
  394.7 33.2 %collective-permute-start.6 = (bf16[2,1,512,512]{3,2,1,0:T(8,128)(2,1)}, bf16[2,1,512,512]{3,2,1,0:T(8,128)(2,1)}, u32[]{:S(2)}, u32[]{:S(2)}) collective-permute-start(bf16[2,1,512,512]{3,2,1,0:T(8,128)(2,1)} %cross.11), channel_id=1, source_target_pairs={{8,16},{16,8},{9,17},{17,9},{10,18},{18,10},{11,19},{19,11},{12,20... | collective-permute-start | bytes 3145736 | tf_op jit(solution)/shard_map/ppermute | solution.py:255
  401.8 122.4 %collective-permute-start.30 = (bf16[2,2,512,512]{3,2,1,0:T(8,128)(2,1)}, bf16[2,2,512,512]{3,2,1,0:T(8,128)(2,1)}, u32[]{:S(2)}, u32[]{:S(2)}) collective-permute-start(bf16[2,2,512,512]{3,2,1,0:T(8,128)(2,1)} %cross.17), channel_id=1, source_target_pairs={{8,16},{16,8},{9,17},{17,9},{10,18},{18,10},{11,19},{19,11},{12,20... | collective-permute-start | bytes 6291464 | tf_op jit(solution)/shard_map/ppermute | solution.py:255
  407.5 25.4 %collective-permute-start.2 = (bf16[2,1,512,512]{3,2,1,0:T(8,128)(2,1)}, bf16[2,1,512,512]{3,2,1,0:T(8,128)(2,1)S(1)}, u32[]{:S(2)}, u32[]{:S(2)}) collective-permute-start(bf16[2,1,512,512]{3,2,1,0:T(8,128)(2,1)} %cross.10), channel_id=1, source_target_pairs={{8,16},{16,8},{9,17},{17,9},{10,18},{18,10},{11,19},{19,11},{12,20... | collective-permute-start | bytes 3145736 | tf_op jit(solution)/shard_map/ppermute | solution.py:255
  411.0 99.1 %collective-permute-start.21 = (bf16[6,4,128,256]{3,2,1,0:T(8,128)(2,1)}, bf16[6,4,128,256]{3,2,1,0:T(8,128)(2,1)}, u32[]{:S(2)}, u32[]{:S(2)}) collective-permute-start(bf16[6,4,128,256]{3,2,1,0:T(8,128)(2,1)} %constant_dynamic-slice_fusion.4), channel_id=1, source_target_pairs={{0,8},{24,16},{1,9},{25,17},{2,10},{26,18},{3,11},{27,19},{4,12},{... | collective-permute-start | bytes 4718600 | tf_op jit(solution)/shard_map/ppermute | solution.py:253
  421.2 14.2 %collective-permute-start.39 = (bf16[1,512,512]{2,1,0:T(8,128)(2,1)}, bf16[1,512,512]{2,1,0:T(8,128)(2,1)}, u32[]{:S(2)}, u32[]{:S(2)}) collective-permute-start(bf16[1,512,512]{2,1,0:T(8,128)(2,1)} %onward.19.mine), channel_id=1, source_target_pairs={{8,0},{16,24},{9,1},{17,25},{10,2},{18,26},{11,3},{19,27},{12,4},{... | collective-permute-start | bytes 1572872 | tf_op jit(solution)/shard_map/ppermute | solution.py:257
  427.9 140.7 %collective-permute-start.26 = (bf16[2,2,512,512]{3,2,1,0:T(8,128)(2,1)}, bf16[2,2,512,512]{3,2,1,0:T(8,128)(2,1)}, u32[]{:S(2)}, u32[]{:S(2)}) collective-permute-start(bf16[2,2,512,512]{3,2,1,0:T(8,128)(2,1)} %cross.16), channel_id=1, source_target_pairs={{8,16},{16,8},{9,17},{17,9},{10,18},{18,10},{11,19},{19,11},{12,20... | collective-permute-start | bytes 6291464 | tf_op jit(solution)/shard_map/ppermute | solution.py:255
  432.9 73.0 %collective-permute-start.35 = (bf16[1,512,512]{2,1,0:T(8,128)(2,1)}, bf16[1,512,512]{2,1,0:T(8,128)(2,1)}, u32[]{:S(2)}, u32[]{:S(2)}) collective-permute-start(bf16[1,512,512]{2,1,0:T(8,128)(2,1)} %onward.18.mine), channel_id=1, source_target_pairs={{8,0},{16,24},{9,1},{17,25},{10,2},{18,26},{11,3},{19,27},{12,4},{... | collective-permute-start | bytes 1572872 | tf_op jit(solution)/shard_map/ppermute | solution.py:257
  435.4 116.9 %collective-permute-start.17 = (bf16[6,4,128,256]{3,2,1,0:T(8,128)(2,1)}, bf16[6,4,128,256]{3,2,1,0:T(8,128)(2,1)}, u32[]{:S(2)}, u32[]{:S(2)}) collective-permute-start(bf16[6,4,128,256]{3,2,1,0:T(8,128)(2,1)} %constant_dynamic-slice_fusion.5), channel_id=1, source_target_pairs={{0,8},{24,16},{1,9},{25,17},{2,10},{26,18},{3,11},{27,19},{4,12},{... | collective-permute-start | bytes 4718600 | tf_op jit(solution)/shard_map/ppermute | solution.py:253
  499.2 15.3 %all-to-all-start.19 = ((bf16[8,1,2,32,512]{4,3,2,1,0:T(8,128)(2,1)}), bf16[8,1,2,32,512]{4,3,2,1,0:T(8,128)(2,1)S(1)}, u32[]{:S(2)}, u32[]{:S(2)}) async-start(bf16[8,1,2,32,512]{4,3,2,1,0:T(8,128)(2,1)} %finish.19), calls=%async_computation.19 | async-start | bytes 1048576 | tf_op jit(solution)/shard_map/all_to_all | solution.py:293
  505.8 22.5 %collective-permute-start.7 = (bf16[1,512,512]{2,1,0:T(8,128)(2,1)}, bf16[1,512,512]{2,1,0:T(8,128)(2,1)}, u32[]{:S(2)}, u32[]{:S(2)}) collective-permute-start(bf16[1,512,512]{2,1,0:T(8,128)(2,1)} %onward.11.mine), channel_id=1, source_target_pairs={{8,0},{16,24},{9,1},{17,25},{10,2},{18,26},{11,3},{19,27},{12,4},{... | collective-permute-start | bytes 1572872 | tf_op jit(solution)/shard_map/ppermute | solution.py:257
  510.1 23.4 %collective-permute-start.3 = (bf16[1,512,512]{2,1,0:T(8,128)(2,1)}, bf16[1,512,512]{2,1,0:T(8,128)(2,1)S(1)}, u32[]{:S(2)}, u32[]{:S(2)}) collective-permute-start(bf16[1,512,512]{2,1,0:T(8,128)(2,1)} %onward.10.mine), channel_id=1, source_target_pairs={{8,0},{16,24},{9,1},{17,25},{10,2},{18,26},{11,3},{19,27},{12,4},{... | collective-permute-start | bytes 1572872 | tf_op jit(solution)/shard_map/ppermute | solution.py:257
  514.6 31.1 %all-to-all-start.17 = ((bf16[8,1,2,32,512]{4,3,2,1,0:T(8,128)(2,1)}), bf16[8,1,2,32,512]{4,3,2,1,0:T(8,128)(2,1)S(1)}, u32[]{:S(2)}, u32[]{:S(2)}) async-start(bf16[8,1,2,32,512]{4,3,2,1,0:T(8,128)(2,1)} %finish.18), calls=%async_computation.17 | async-start | bytes 1048576 | tf_op jit(solution)/shard_map/all_to_all | solution.py:293
  524.2 83.7 %collective-permute-start.22 = (bf16[2,2,512,512]{3,2,1,0:T(8,128)(2,1)}, bf16[2,2,512,512]{3,2,1,0:T(8,128)(2,1)S(1)}, u32[]{:S(2)}, u32[]{:S(2)}) collective-permute-start(bf16[2,2,512,512]{3,2,1,0:T(8,128)(2,1)} %cross.15), channel_id=1, source_target_pairs={{8,16},{16,8},{9,17},{17,9},{10,18},{18,10},{11,19},{19,11},{12,20... | collective-permute-start | bytes 6291464 | tf_op jit(solution)/shard_map/ppermute | solution.py:255
  528.4 56.8 %collective-permute-start.31 = (bf16[2,512,512]{2,1,0:T(8,128)(2,1)}, bf16[2,512,512]{2,1,0:T(8,128)(2,1)}, u32[]{:S(2)}, u32[]{:S(2)}) collective-permute-start(bf16[2,512,512]{2,1,0:T(8,128)(2,1)} %onward.17.mine), channel_id=1, source_target_pairs={{8,0},{16,24},{9,1},{17,25},{10,2},{18,26},{11,3},{19,27},{12,4},{... | collective-permute-start | bytes 3145736 | tf_op jit(solution)/shard_map/ppermute | solution.py:257
  533.5 67.0 %collective-permute-start.13 = (bf16[6,4,128,256]{3,2,1,0:T(8,128)(2,1)}, bf16[6,4,128,256]{3,2,1,0:T(8,128)(2,1)}, u32[]{:S(2)}, u32[]{:S(2)}) collective-permute-start(bf16[6,4,128,256]{3,2,1,0:T(8,128)(2,1)} %constant_dynamic-slice_fusion.6), channel_id=1, source_target_pairs={{0,8},{24,16},{1,9},{25,17},{2,10},{26,18},{3,11},{27,19},{4,12},{... | collective-permute-start | bytes 4718600 | tf_op jit(solution)/shard_map/ppermute | solution.py:253
  545.7 13.9 %all-to-all-start.3 = ((bf16[8,1,2,32,512]{4,3,2,1,0:T(8,128)(2,1)}), bf16[8,1,2,32,512]{4,3,2,1,0:T(8,128)(2,1)S(1)}, u32[]{:S(2)}, u32[]{:S(2)}) async-start(bf16[8,1,2,32,512]{4,3,2,1,0:T(8,128)(2,1)} %finish.11), calls=%async_computation.3 | async-start | bytes 1048576 | tf_op jit(solution)/shard_map/all_to_all | solution.py:293
  552.3 28.9 %collective-permute-start.12 = (bf16[4,256,128]{2,1,0:T(8,128)(2,1)S(1)}, bf16[4,256,128]{2,1,0:T(8,128)(2,1)}, u32[]{:S(2)}, u32[]{:S(2)}) collective-permute-start(bf16[4,256,128]{2,1,0:T(8,128)(2,1)S(1)} %fusion.69.own_rows), channel_id=1, source_target_pairs={{0,8},{24,16},{1,9},{25,17},{2,10},{26,18},{3,11},{27,19},{4,12},{... | collective-permute-start | bytes 786440 | tf_op jit(solution)/shard_map/ppermute | solution.py:252
  559.6 36.2 %all-to-all-start.1 = ((bf16[8,1,2,32,512]{4,3,2,1,0:T(8,128)(2,1)}), bf16[8,1,2,32,512]{4,3,2,1,0:T(8,128)(2,1)S(1)}, u32[]{:S(2)}, u32[]{:S(2)}) async-start(bf16[8,1,2,32,512]{4,3,2,1,0:T(8,128)(2,1)} %finish.10), calls=%async_computation.1 | async-start | bytes 1048576 | tf_op jit(solution)/shard_map/all_to_all | solution.py:293
  568.6 75.0 %collective-permute-start.18 = (bf16[2,2,512,512]{3,2,1,0:T(8,128)(2,1)}, bf16[2,2,512,512]{3,2,1,0:T(8,128)(2,1)}, u32[]{:S(2)}, u32[]{:S(2)}) collective-permute-start(bf16[2,2,512,512]{3,2,1,0:T(8,128)(2,1)} %cross.14), channel_id=1, source_target_pairs={{8,16},{16,8},{9,17},{17,9},{10,18},{18,10},{11,19},{19,11},{12,20... | collective-permute-start | bytes 6291464 | tf_op jit(solution)/shard_map/ppermute | solution.py:255
  581.1 32.7 %collective-permute-start.27 = (bf16[2,512,512]{2,1,0:T(8,128)(2,1)}, bf16[2,512,512]{2,1,0:T(8,128)(2,1)}, u32[]{:S(2)}, u32[]{:S(2)}) collective-permute-start(bf16[2,512,512]{2,1,0:T(8,128)(2,1)} %onward.16.mine), channel_id=1, source_target_pairs={{8,0},{16,24},{9,1},{17,25},{10,2},{18,26},{11,3},{19,27},{12,4},{... | collective-permute-start | bytes 3145736 | tf_op jit(solution)/shard_map/ppermute | solution.py:257
  585.1 51.3 %collective-permute-start.9 = (bf16[6,4,128,256]{3,2,1,0:T(8,128)(2,1)}, bf16[6,4,128,256]{3,2,1,0:T(8,128)(2,1)}, u32[]{:S(2)}, u32[]{:S(2)}) collective-permute-start(bf16[6,4,128,256]{3,2,1,0:T(8,128)(2,1)} %constant_dynamic-slice_fusion.7), channel_id=1, source_target_pairs={{0,8},{24,16},{1,9},{25,17},{2,10},{26,18},{3,11},{27,19},{4,12},{... | collective-permute-start | bytes 4718600 | tf_op jit(solution)/shard_map/ppermute | solution.py:253
  596.6 21.2 %all-to-all-start.15 = ((bf16[8,2,2,32,512]{4,3,2,1,0:T(8,128)(2,1)}), bf16[8,2,2,32,512]{4,3,2,1,0:T(8,128)(2,1)S(1)}, u32[]{:S(2)}, u32[]{:S(2)}) async-start(bf16[8,2,2,32,512]{4,3,2,1,0:T(8,128)(2,1)} %finish.17), calls=%async_computation.15 | async-start | bytes 2097152 | tf_op jit(solution)/shard_map/all_to_all | solution.py:293
  605.9 50.6 %collective-permute-start.14 = (bf16[2,2,512,512]{3,2,1,0:T(8,128)(2,1)}, bf16[2,2,512,512]{3,2,1,0:T(8,128)(2,1)}, u32[]{:S(2)}, u32[]{:S(2)}) collective-permute-start(bf16[2,2,512,512]{3,2,1,0:T(8,128)(2,1)} %cross.13), channel_id=1, source_target_pairs={{8,16},{16,8},{9,17},{17,9},{10,18},{18,10},{11,19},{19,11},{12,20... | collective-permute-start | bytes 6291464 | tf_op jit(solution)/shard_map/ppermute | solution.py:255
  612.5 35.7 %collective-permute-start.23 = (bf16[2,512,512]{2,1,0:T(8,128)(2,1)}, bf16[2,512,512]{2,1,0:T(8,128)(2,1)}, u32[]{:S(2)}, u32[]{:S(2)}) collective-permute-start(bf16[2,512,512]{2,1,0:T(8,128)(2,1)} %onward.15.mine), channel_id=1, source_target_pairs={{8,0},{16,24},{9,1},{17,25},{10,2},{18,26},{11,3},{19,27},{12,4},{... | collective-permute-start | bytes 3145736 | tf_op jit(solution)/shard_map/ppermute | solution.py:257
  617.8 34.4 %all-to-all-start.13 = ((bf16[8,2,2,32,512]{4,3,2,1,0:T(8,128)(2,1)}), bf16[8,2,2,32,512]{4,3,2,1,0:T(8,128)(2,1)}, u32[]{:S(2)}, u32[]{:S(2)}) async-start(bf16[8,2,2,32,512]{4,3,2,1,0:T(8,128)(2,1)} %finish.16), calls=%async_computation.13 | async-start | bytes 2097152 | tf_op jit(solution)/shard_map/all_to_all | solution.py:293
  624.4 12.0 %collective-permute-start.8 = (bf16[4,256,128]{2,1,0:T(8,128)(2,1)S(1)}, bf16[4,256,128]{2,1,0:T(8,128)(2,1)S(1)}, u32[]{:S(2)}, u32[]{:S(2)}) collective-permute-start(bf16[4,256,128]{2,1,0:T(8,128)(2,1)S(1)} %fusion.66.own_rows), channel_id=1, source_target_pairs={{0,8},{24,16},{1,9},{25,17},{2,10},{26,18},{3,11},{27,19},{4,12},{... | collective-permute-start | bytes 786440 | tf_op jit(solution)/shard_map/ppermute | solution.py:252
  642.6 42.7 %collective-permute-start.10 = (bf16[2,2,512,512]{3,2,1,0:T(8,128)(2,1)}, bf16[2,2,512,512]{3,2,1,0:T(8,128)(2,1)S(1)}, u32[]{:S(2)}, u32[]{:S(2)}) collective-permute-start(bf16[2,2,512,512]{3,2,1,0:T(8,128)(2,1)} %cross.12), channel_id=1, source_target_pairs={{8,16},{16,8},{9,17},{17,9},{10,18},{18,10},{11,19},{19,11},{12,20... | collective-permute-start | bytes 6291464 | tf_op jit(solution)/shard_map/ppermute | solution.py:255
  646.9 30.1 %collective-permute-start.19 = (bf16[2,512,512]{2,1,0:T(8,128)(2,1)}, bf16[2,512,512]{2,1,0:T(8,128)(2,1)}, u32[]{:S(2)}, u32[]{:S(2)}) collective-permute-start(bf16[2,512,512]{2,1,0:T(8,128)(2,1)} %onward.14.mine), channel_id=1, source_target_pairs={{8,0},{16,24},{9,1},{17,25},{10,2},{18,26},{11,3},{19,27},{12,4},{... | collective-permute-start | bytes 3145736 | tf_op jit(solution)/shard_map/ppermute | solution.py:257
  652.2 28.8 %all-to-all-start.11 = ((bf16[8,2,2,32,512]{4,3,2,1,0:T(8,128)(2,1)}), bf16[8,2,2,32,512]{4,3,2,1,0:T(8,128)(2,1)}, u32[]{:S(2)}, u32[]{:S(2)}) async-start(bf16[8,2,2,32,512]{4,3,2,1,0:T(8,128)(2,1)} %finish.15), calls=%async_computation.11 | async-start | bytes 2097152 | tf_op jit(solution)/shard_map/all_to_all | solution.py:293
  659.8 38.4 %collective-permute-start.15 = (bf16[2,512,512]{2,1,0:T(8,128)(2,1)}, bf16[2,512,512]{2,1,0:T(8,128)(2,1)}, u32[]{:S(2)}, u32[]{:S(2)}) collective-permute-start(bf16[2,512,512]{2,1,0:T(8,128)(2,1)} %onward.13.mine), channel_id=1, source_target_pairs={{8,0},{16,24},{9,1},{17,25},{10,2},{18,26},{11,3},{19,27},{12,4},{... | collective-permute-start | bytes 3145736 | tf_op jit(solution)/shard_map/ppermute | solution.py:257
  681.0 21.2 %all-to-all-start.9 = ((bf16[8,2,2,32,512]{4,3,2,1,0:T(8,128)(2,1)}), bf16[8,2,2,32,512]{4,3,2,1,0:T(8,128)(2,1)}, u32[]{:S(2)}, u32[]{:S(2)}) async-start(bf16[8,2,2,32,512]{4,3,2,1,0:T(8,128)(2,1)} %finish.14), calls=%async_computation.9 | async-start | bytes 2097152 | tf_op jit(solution)/shard_map/all_to_all | solution.py:293
  689.9 52.1 %collective-permute-start.11 = (bf16[2,512,512]{2,1,0:T(8,128)(2,1)}, bf16[2,512,512]{2,1,0:T(8,128)(2,1)S(1)}, u32[]{:S(2)}, u32[]{:S(2)}) collective-permute-start(bf16[2,512,512]{2,1,0:T(8,128)(2,1)} %onward.12.mine), channel_id=1, source_target_pairs={{8,0},{16,24},{9,1},{17,25},{10,2},{18,26},{11,3},{19,27},{12,4},{... | collective-permute-start | bytes 3145736 | tf_op jit(solution)/shard_map/ppermute | solution.py:257
  702.2 44.8 %all-to-all-start.7 = ((bf16[8,2,2,32,512]{4,3,2,1,0:T(8,128)(2,1)}), bf16[8,2,2,32,512]{4,3,2,1,0:T(8,128)(2,1)S(1)}, u32[]{:S(2)}, u32[]{:S(2)}) async-start(bf16[8,2,2,32,512]{4,3,2,1,0:T(8,128)(2,1)} %finish.13), calls=%async_computation.7 | async-start | bytes 2097152 | tf_op jit(solution)/shard_map/all_to_all | solution.py:293
  747.0 23.7 %all-to-all-start.5 = ((bf16[8,2,2,32,512]{4,3,2,1,0:T(8,128)(2,1)}), bf16[8,2,2,32,512]{4,3,2,1,0:T(8,128)(2,1)S(1)}, u32[]{:S(2)}, u32[]{:S(2)}) async-start(bf16[8,2,2,32,512]{4,3,2,1,0:T(8,128)(2,1)} %finish.12), calls=%async_computation.5 | async-start | bytes 2097152 | tf_op jit(solution)/shard_map/all_to_all | solution.py:293
  (37 other events, 323.2 us)
